TPU v7x, 128 devices: a whole 4x4x4 slice. The times are simulated.
128 devices in a mesh: sp: 8 (over z, core), tp: 16 (over x, y).
Axes of the slice: x: 4, y: 4, z: 4, core: 2. Of those that a mesh axis runs over, the one named last changes fastest.
Arguments:
- tokens: bfloat16 [16384, 2048], P(('sp', 'tp')), may hold values from -3 to 3
- queries: bfloat16 [16384, 2048], P(('sp', 'tp')), may hold values from -140 to 140
- keys: bfloat16 [16384, 1024], P(('sp', 'tp')), may hold values from -6 to 6
- values: bfloat16 [16384, 1024], P(('sp', 'tp')), may hold values from -6 to 6
- out_weight: bfloat16 [2048, 2048], P('sp', 'tp'), may hold values from -0.25 to 0.25
- norm_gain: bfloat16 [2048], replicated, may hold values from 0.099609375 to 1.8984375
- gate_weight: bfloat16 [2048, 7168], P('sp', 'tp'), may hold values from -0.125 to 0.125
- up_weight: bfloat16 [2048, 7168], P('sp', 'tp'), may hold values from -0.125 to 0.125
- down_weight: bfloat16 [7168, 2048], P('tp', 'sp'), may hold values from -0.125 to 0.125
Outputs:
- attended: bfloat16 [16384, 2048], P(('sp', 'tp'))
- layer_out: bfloat16 [16384, 2048], P(('sp', 'tp'))
All inputs are finite; a program needn't handle non-finite values.
Results may differ from a plain program's by a relative error of at most 0.023.
Values may be sent and summed in bfloat16 or wider, within the bound.
No kernel may reach another device: no remote copies, remote signals or barrier semaphores. Data moves between devices by JAX's collectives and lax.ppermute only.
A program may use at most 128 MiB of HBM per device.

v0:
```python
import jax
import jax.numpy as jnp
from jax import lax
from jax.sharding import PartitionSpec as P

HEAD_DIM = 128
norm_eps = 1e-05


def side_by_side(arrays, axis, dim, along):
    both = jnp.concatenate(arrays, axis=along)
    result, at, done = (lax.all_gather(both, axis, axis=dim, tiled=True), 0, [])
    for a in arrays:
        done.append(lax.slice_in_dim(result, at, at + a.shape[along], axis=along))
        at += a.shape[along]
    return tuple(done)


def sent_to_all(array, axis):
    copies = jnp.broadcast_to(array, (lax.axis_size(axis), *array.shape))
    return lax.all_to_all(copies, axis, split_axis=0, concat_axis=0, tiled=True)


def joined_along(blocks, dim):
    dims = list(blocks.shape[1:])
    dims[dim] *= blocks.shape[0]
    return jnp.moveaxis(blocks, 0, dim).reshape(dims)


def gather_directly(array, axis, dim):
    blocks = sent_to_all(array, axis)
    return joined_along(blocks, dim)


def attend(q_block, query_pos, k_block, v_block, key_pos, kv_local):
    row_count = q_block.shape[0]
    key_count = k_block.shape[0]
    q_four = q_block.reshape(row_count, kv_local, -1, HEAD_DIM)
    k_three = k_block.reshape(key_count, kv_local, HEAD_DIM)
    v_three = v_block.reshape(key_count, kv_local, HEAD_DIM)
    scores = jnp.einsum(
        "qhgd,khd->hgqk", q_four, k_three, preferred_element_type=jnp.float32
    ) * HEAD_DIM ** (-0.5)
    causal = key_pos[None, :] <= query_pos[:, None]
    scores = jnp.where(causal[None, None, :, :], scores, -1e30)
    row_peak = jnp.max(scores, axis=-1, keepdims=True)
    exp_terms = jnp.exp(scores - row_peak)
    probs = (exp_terms / jnp.sum(exp_terms, axis=-1, keepdims=True)).astype(jnp.bfloat16)
    mixed_out = jnp.einsum("hgqk,khd->qhgd", probs, v_three, preferred_element_type=jnp.float32)
    return mixed_out.astype(jnp.bfloat16).reshape(row_count, -1)


def add_rows(all_rows, weight_piece):
    return jnp.dot(all_rows, weight_piece, preferred_element_type=jnp.float32)


def shards(
    tokens, queries, keys, values, out_weight, norm_gain, gate_weight, up_weight, down_weight
):
    shard_rows = tokens.shape[0]
    sp_count = lax.axis_size("sp")
    tp_count = lax.axis_size("tp")
    segment_len = shard_rows * tp_count
    seq_len = segment_len * sp_count
    local_q = lax.all_to_all(queries, "sp", split_axis=1, concat_axis=0, tiled=True)
    part_keys, part_values = (
        lax.all_to_all(keys, "sp", split_axis=1, concat_axis=0, tiled=True),
        lax.all_to_all(values, "sp", split_axis=1, concat_axis=0, tiled=True),
    )
    width_kv = part_keys.shape[1]
    grid_keys, grid_values = side_by_side(
        (
            part_keys.reshape(sp_count, shard_rows, width_kv),
            part_values.reshape(sp_count, shard_rows, width_kv),
        ),
        "tp",
        1,
        0,
    )
    all_keys = grid_keys.reshape(seq_len, width_kv)
    all_values = grid_values.reshape(seq_len, width_kv)
    kv_local = all_keys.shape[1] // HEAD_DIM
    query_index = jnp.arange(sp_count * shard_rows, dtype=jnp.int32)
    query_pos = (
        query_index // shard_rows * segment_len
        + lax.axis_index("tp") * shard_rows
        + query_index % shard_rows
    )
    key_pos = jnp.arange(seq_len, dtype=jnp.int32)
    pieces_out = []
    for segment in range(sp_count):
        first_row = segment * shard_rows
        key_reach = (segment + 1) * segment_len
        pieces_out.append(
            attend(
                local_q[first_row : first_row + shard_rows],
                query_pos[first_row : first_row + shard_rows],
                all_keys[:key_reach],
                all_values[:key_reach],
                key_pos[:key_reach],
                kv_local,
            )
        )
    attn = jnp.concatenate(pieces_out, axis=0)
    wo_full = lax.all_gather(out_weight, "tp", axis=1, tiled=True)
    block_rows = attn
    attn_part = lax.psum_scatter(
        jnp.dot(block_rows, wo_full, preferred_element_type=jnp.float32).astype(jnp.bfloat16),
        "sp",
        scatter_dimension=0,
        tiled=True,
    ).astype(jnp.float32)
    attended = (tokens.astype(jnp.float32) + attn_part).astype(jnp.bfloat16)
    attended_wide = attended.astype(jnp.float32)
    inverse_rms = lax.rsqrt(
        jnp.mean(attended_wide * attended_wide, axis=1, keepdims=True) + norm_eps
    )
    normed = (attended_wide * inverse_rms * norm_gain.astype(jnp.float32)).astype(jnp.bfloat16)
    all_rows = lax.all_gather(normed, "tp", axis=0, tiled=True)

    def add_single(weight_piece):
        return add_rows(all_rows, weight_piece)

    gate_sum = add_single(gather_directly(gate_weight, "sp", 0))
    up_sum = add_single(lax.all_gather(up_weight, "sp", axis=0, tiled=True))
    hidden = (jax.nn.silu(gate_sum) * up_sum).astype(jnp.bfloat16)
    down_full = lax.all_gather(down_weight, "sp", axis=1, tiled=True)
    block_rows = hidden
    ffn_part = lax.psum_scatter(
        jnp.dot(block_rows, down_full, preferred_element_type=jnp.float32).astype(jnp.bfloat16),
        "tp",
        scatter_dimension=0,
        tiled=True,
    ).astype(jnp.float32)
    layer_out = (attended_wide + ffn_part).astype(jnp.bfloat16)
    return (attended, layer_out)


def solution(mesh):
    return jax.shard_map(
        shards,
        mesh=mesh,
        in_specs=(
            P(("sp", "tp"), None),
            P(("sp", "tp"), None),
            P(("sp", "tp"), None),
            P(("sp", "tp"), None),
            P("sp", "tp"),
            P(),
            P("sp", "tp"),
            P("sp", "tp"),
            P("tp", "sp"),
        ),
        out_specs=(P(("sp", "tp"), None), P(("sp", "tp"), None)),
        check_vma=False,
    )
```

profile of v0, /device:TPU:0, one launch (start us, length us, event | category | flops | bytes accessed | tf_op | source)
XLA Modules:
  0.0 448.6 jit_solution(11308070882767555244)
XLA Ops:
  9.2 5.4 %all-to-all-start.1 = ((bf16[128,8,128]{2,0,1:T(8,128)(2,1)}), bf16[128,8,128]{2,0,1:T(8,128)(2,1)S(1)}, u32[]{:S(2)}, u32[]{:S(2)}) async-start(bf16[128,8,128]{2,0,1:T(8,128)(2,1)} %copy.90), calls=%async_computation.1 | async-start | bytes 524288 | tf_op jit(solution)/shard_map/all_to_all | solution.py:68
  16.0 6.1 %all-to-all-done.1 = bf16[128,8,128]{2,0,1:T(8,128)(2,1)S(1)} async-done(((bf16[128,8,128]{2,0,1:T(8,128)(2,1)}), bf16[128,8,128]{2,0,1:T(8,128)(2,1)S(1)}, u32[]{:S(2)}, u32[]{:S(2)}) %all-to-all-start.1) | async-done | bytes 262176 | tf_op jit(solution)/shard_map/all_to_all | solution.py:68
  22.1 9.9 %all_to_all.53 = bf16[128,8,128]{2,0,1:T(8,128)(2,1)S(1)} all-to-all(bf16[128,8,128]{2,0,1:T(8,128)(2,1)S(1)} %copy.88), channel_id=1, replica_groups=mesh['sp'=8,'tp'=16] {'sp'}, dimensions={1} | all-to-all | bytes 524288 | tf_op jit(solution)/shard_map/all_to_all | solution.py:67
  33.9 3.5 all-to-all-start.2
  38.3 2.4 iota_compare_fusion
  42.6 3.4 broadcast_compare_fusion.4
  46.0 4.4 broadcast_compare_fusion.3
  50.4 5.5 %broadcast_compare_fusion.2 = pred[128,10240]{0,1:T(8,128)(4,1)} fusion(s32[128]{0:T(128)S(1)} %get-tuple-element.29, s32[10240]{0:T(1024)S(1)} %iota_add_fusion.2), kind=kLoop, calls=%fused_computation.62 | loop fusion | flops 1310720 | bytes 1352192 | tf_op jit(solution)/shard_map/le | solution.py:44
  55.9 6.4 %broadcast_compare_fusion.1 = pred[128,12288]{0,1:T(8,128)(4,1)} fusion(s32[128]{0:T(128)S(1)} %get-tuple-element.28, s32[12288]{0:T(1024)S(1)} %iota_add_fusion.1), kind=kLoop, calls=%fused_computation.59 | loop fusion | flops 1572864 | bytes 1622528 | tf_op jit(solution)/shard_map/le | solution.py:44
  62.3 6.7 %broadcast_compare_fusion = pred[128,14336]{0,1:T(8,128)(4,1)S(1)} fusion(s32[128]{0:T(128)S(1)} %get-tuple-element.27, s32[14336]{0:T(1024)S(1)} %iota_add_fusion), kind=kLoop, calls=%fused_computation.56 | loop fusion | flops 1835008 | bytes 1892864 | tf_op jit(solution)/shard_map/le | solution.py:44
  70.1 33.2 %all-gather.6.cloned.1.call-done = bf16[16,2048,128]{2,1,0:T(8,128)(2,1)} async-done(((bf16[16,128,128]{2,1,0:T(8,128)(2,1)}), bf16[16,2048,128]{2,1,0:T(8,128)(2,1)}) %all-gather.6.cloned.1.call-update) | async-done | bytes 8388624 | tf_op jit(solution)/shard_map/all_gather | solution.py:12
  123.1 2.2 fusion.87
  130.2 2.7 fusion.88
  134.7 2.5 fusion.50
  137.7 6.8 %fusion.89 = (f32[2,128]{1,0:T(2,128)S(1)}, f32[1,2,128,14336]{2,3,1,0:T(8,128)}) fusion(bf16[14336,128,1]{1,0,2:T(8,128)(2,1)S(1)} %bitcast.229, bf16[128,2,128]{0,2,1:T(8,128)(2,1)S(1)} %bitcast.247, pred[128,14336]{0,1:T(8,128)(4,1)S(1)} %broadcast_compare_fusion), kind=kOutput, calls=%fused_computation.138 | convolution fusion | flops 950533888 | bytes 20251648 | tf_op jit(solution)/shard_map/qhgd,khd->hgqk/dot_general | solution.py:41
  144.6 7.4 %fusion.8 = f32[2,128]{1,0:T(2,128)S(1)} fusion(f32[1,2,128,14336]{2,3,1,0:T(8,128)} %get-tuple-element.47, f32[2,128]{1,0:T(2,128)S(1)} %get-tuple-element.46), kind=kLoop, calls=%fused_computation.16 | loop fusion | flops 7339776 | bytes 14682112 | tf_op jit(solution)/shard_map/reduce_sum | solution.py:48
  152.0 6.9 %fusion.53 = bf16[128,2,128]{2,0,1:T(8,128)(2,1)S(1)} fusion(bf16[14336,128,1]{1,0,2:T(8,128)(2,1)S(1)} %bitcast.228, f32[2,128]{1,0:T(2,128)S(1)} %fusion.8, f32[1,2,128,14336]{2,3,1,0:T(8,128)} %get-tuple-element.47, f32[2,128]{1,0:T(2,128)S(1)} %get-tuple-element.46), kind=kOutput, calls=%fused_computation.79 | convolution fusion | flops 950566912 | bytes 18417664 | tf_op jit(solution)/shard_map/hgqk,khd->qhgd/dot_general | solution.py:49
  158.9 2.2 fusion.74
  161.2 5.2 %fusion.90 = (f32[2,128]{1,0:T(2,128)S(1)}, f32[1,2,128,16384]{2,3,1,0:T(8,128)S(1)}) fusion(bf16[16384,128,1]{1,0,2:T(8,128)(2,1)} %bitcast.227, bf16[128,2,128]{0,2,1:T(8,128)(2,1)S(1)} %bitcast.246, pred[128,16384]{0,1:T(8,128)(4,1)S(1)} %copy-done.2), kind=kOutput, calls=%fused_computation.139 | convolution fusion | flops 1086324480 | bytes 23135232 | tf_op jit(solution)/shard_map/qhgd,khd->hgqk/dot_general | solution.py:41
  166.4 4.4 fusion.6
  170.8 3.2 fusion.56
  174.1 4.5 %convolution_convert_fusion.1 = bf16[1024,2048]{1,0:T(8,128)(2,1)} fusion(bf16[1024,256]{0,1:T(8,128)(2,1)S(1)} %constant_dynamic-update-slice_fusion, bf16[256,2048]{1,0:T(8,128)(2,1)} %all-gather.8.cloned.1.call-done), kind=kOutput, calls=%fused_computation.53 | convolution fusion | flops 1075838976 | bytes 5767168 | tf_op jit(solution)/shard_map/dot_general | solution.py:108
  178.7 37.9 %reduce-scatter.3.cloned.1.call-done = bf16[128,2048]{1,0:T(8,128)(2,1)} async-done(((bf16[1024,2048]{1,0:T(8,128)(2,1)}), bf16[128,2048]{1,0:T(8,128)(2,1)}) %reduce-scatter.3.cloned.1.call-update) | async-done | bytes 524304 | tf_op jit(solution)/shard_map/reduce_scatter | solution.py:107
  221.0 3.6 all-to-all-start.3
  225.4 23.5 %all-to-all-done.3 = bf16[8,256,448]{1,2,0:T(8,128)(2,1)S(1)} async-done(((bf16[8,256,448]{1,2,0:T(8,128)(2,1)}), bf16[8,256,448]{1,2,0:T(8,128)(2,1)S(1)}, u32[]{:S(2)}, u32[]{:S(2)}) %all-to-all-start.3) | async-done | bytes 1835040 | tf_op jit(solution)/shard_map/all_to_all | solution.py:21
  250.3 38.4 %all-gather.10.cloned.1.call-done = bf16[2048,2048]{1,0:T(8,128)(2,1)} async-done(((bf16[128,2048]{1,0:T(8,128)(2,1)}), bf16[2048,2048]{1,0:T(8,128)(2,1)}) %all-gather.10.cloned.1.call-update) | async-done | bytes 8388624 | tf_op jit(solution)/shard_map/all_gather | solution.py:119
  288.7 9.7 %fusion.91 = f32[2048,448]{0,1:T(8,128)} fusion(bf16[2048,2048]{1,0:T(8,128)(2,1)} %all-gather.10.cloned.1.call-done, bf16[2048,448]{0,1:T(8,128)(2,1)} %bitcast.237), kind=kOutput, calls=%fused_computation.140 | convolution fusion | flops 3758096384 | bytes 13893632 | tf_op jit(solution)/shard_map/dot_general | solution.py:54
  298.4 17.6 %all-gather.12.cloned.1.call-done = bf16[2048,448]{0,1:T(8,128)(2,1)} async-done(((bf16[256,448]{0,1:T(8,128)(2,1)}), bf16[2048,448]{0,1:T(8,128)(2,1)}) %all-gather.12.cloned.1.call-update) | async-done | bytes 1835024 | tf_op jit(solution)/shard_map/all_gather | solution.py:125
  316.1 9.1 %multiply_convert_fusion = bf16[2048,448]{0,1:T(8,128)(2,1)S(1)} fusion(f32[2048,448]{0,1:T(8,128)} %fusion.91, bf16[2048,2048]{1,0:T(8,128)(2,1)} %all-gather.10.cloned.1.call-done, bf16[2048,448]{0,1:T(8,128)(2,1)} %all-gather.12.cloned.1.call-done), kind=kOutput, calls=%fused_computation.55 | convolution fusion | flops 3763601408 | bytes 15728640 | tf_op jit(solution)/shard_map/dot_general | solution.py:54
  325.2 19.3 %all-gather.14.cloned.1.call-done = bf16[448,2048]{1,0:T(8,128)(2,1)} async-done(((bf16[448,256]{1,0:T(8,128)(2,1)}), bf16[448,2048]{1,0:T(8,128)(2,1)}) %all-gather.14.cloned.1.call-update) | async-done | bytes 1835024 | tf_op jit(solution)/shard_map/all_gather | solution.py:127
  344.5 8.3 %convolution_convert_fusion = bf16[2048,2048]{1,0:T(8,128)(2,1)} fusion(bf16[2048,448]{0,1:T(8,128)(2,1)S(1)} %multiply_convert_fusion, bf16[448,2048]{1,0:T(8,128)(2,1)} %all-gather.14.cloned.1.call-done), kind=kOutput, calls=%fused_computation.34 | convolution fusion | flops 3762290688 | bytes 12058624 | tf_op jit(solution)/shard_map/dot_general | solution.py:130
  352.8 86.9 %reduce-scatter.5.cloned.1.call-done = bf16[128,2048]{1,0:T(8,128)(2,1)} async-done(((bf16[2048,2048]{1,0:T(8,128)(2,1)}), bf16[128,2048]{1,0:T(8,128)(2,1)}) %reduce-scatter.5.cloned.1.call-update) | async-done | bytes 524304 | tf_op jit(solution)/shard_map/reduce_scatter | solution.py:129
  (104 shorter events, 44.6 us)
Async XLA Ops:
  7.2 25.7 %copy-start.7 = (bf16[128,2048]{1,0:T(8,128)(2,1)S(1)}, bf16[128,2048]{1,0:T(8,128)(2,1)}, u32[]{:S(2)}) copy-start(bf16[128,2048]{1,0:T(8,128)(2,1)} %param.10) | copy-start | bytes 1572868
  9.2 12.9 %all-to-all-start.1 = ((bf16[128,8,128]{2,0,1:T(8,128)(2,1)}), bf16[128,8,128]{2,0,1:T(8,128)(2,1)S(1)}, u32[]{:S(2)}, u32[]{:S(2)}) async-start(bf16[128,8,128]{2,0,1:T(8,128)(2,1)} %copy.90), calls=%async_computation.1 | async-start | bytes 524288 | tf_op jit(solution)/shard_map/all_to_all | solution.py:68
  14.6 88.6 %all-gather.6.cloned.1.call-start = ((), (), s32[]{:S(2)}) async-start(), calls=%async_computation.6 | async-start | bytes 8912896 | tf_op jit(solution)/shard_map/all_gather | solution.py:12
  33.9 35.4 %all-to-all-start.2 = ((bf16[128,8,256]{0,2,1:T(8,128)(2,1)}), bf16[128,8,256]{0,2,1:T(8,128)(2,1)S(1)}, u32[]{:S(2)}, u32[]{:S(2)}) async-start(bf16[128,8,256]{0,2,1:T(8,128)(2,1)} %bitcast.8), calls=%async_computation.2 | async-start | bytes 1048576 | tf_op jit(solution)/shard_map/all_to_all | solution.py:65
  37.4 136.7 %all-gather.8.cloned.1.call-start = ((), (), s32[]{:S(2)}) async-start(), calls=%async_computation.7 | async-start | bytes 1114112 | tf_op jit(solution)/shard_map/all_gather | solution.py:105
  38.2 178.5 %reduce-scatter.3.cloned.1.call-start = ((), (), s32[]{:S(2)}) async-start(), calls=%async_computation.8 | async-start | bytes 4718592 | tf_op jit(solution)/shard_map/reduce_scatter | solution.py:107
  105.1 3.5 copy-start
  106.8 1.9 copy-start.15
  111.2 1.1 copy-start.6
  111.2 1.1 copy-start.14
  115.9 1.2 copy-start.5
  115.9 1.2 copy-start.13
  121.7 1.3 copy-start.4
  121.8 1.3 copy-start.12
  128.8 1.4 copy-start.3
  128.8 1.4 copy-start.11
  158.9 2.3 copy-start.2
  158.9 2.3 copy-start.10
  174.1 4.6 %copy-start.16 = (bf16[2048]{0:T(1024)(128)(2,1)S(1)}, bf16[2048]{0:T(1024)(128)(2,1)}, u32[]{:S(2)}) copy-start(bf16[2048]{0:T(1024)(128)(2,1)} %param.14) | copy-start | bytes 12292
  174.1 42.6 %copy-start.8 = (bf16[128,2048]{1,0:T(8,128)(2,1)S(1)}, bf16[128,2048]{1,0:T(8,128)(2,1)}, u32[]{:S(2)}) copy-start(bf16[128,2048]{1,0:T(8,128)(2,1)} %param.9) | copy-start | bytes 1572868
  178.6 40.9 %copy-start.9 = (bf16[256,448]{0,1:T(8,128)(2,1)S(1)}, bf16[256,448]{0,1:T(8,128)(2,1)}, u32[]{:S(2)}) copy-start(bf16[256,448]{0,1:T(8,128)(2,1)} %param.15) | copy-start | bytes 688132
  178.6 110.1 %all-gather.10.cloned.1.call-start = ((), (), s32[]{:S(2)}) async-start(), calls=%async_computation.9 | async-start | bytes 8912896 | tf_op jit(solution)/shard_map/all_gather | solution.py:119
  217.9 221.7 %copy-start.1 = (bf16[128,2048]{1,0:T(8,128)(2,1)}, bf16[128,2048]{1,0:T(8,128)(2,1)S(1)}, u32[]{:S(2)}) copy-start(bf16[128,2048]{1,0:T(8,128)(2,1)S(1)} %get-tuple-element.3) | copy-start | bytes 1572868
  219.0 97.1 %all-gather.12.cloned.1.call-start = ((), (), s32[]{:S(2)}) async-start(), calls=%async_computation.10 | async-start | bytes 2064384 | tf_op jit(solution)/shard_map/all_gather | solution.py:125
  221.0 27.9 %all-to-all-start.3 = ((bf16[8,256,448]{1,2,0:T(8,128)(2,1)}), bf16[8,256,448]{1,2,0:T(8,128)(2,1)S(1)}, u32[]{:S(2)}, u32[]{:S(2)}) async-start(bf16[8,256,448]{1,2,0:T(8,128)(2,1)} %broadcast_in_dim.157), calls=%async_computation.4 | async-start | bytes 3670016 | tf_op jit(solution)/shard_map/all_to_all | solution.py:21
  224.6 119.9 %all-gather.14.cloned.1.call-start = ((), (), s32[]{:S(2)}) async-start(), calls=%async_computation.11 | async-start | bytes 2064384 | tf_op jit(solution)/shard_map/all_gather | solution.py:127
  225.2 214.5 %reduce-scatter.5.cloned.1.call-start = ((), (), s32[]{:S(2)}) async-start(), calls=%async_computation.12 | async-start | bytes 8912896 | tf_op jit(solution)/shard_map/reduce_scatter | solution.py:129
Sparse Core Ops, SparseCore 0:
  33.0 70.1 all-gather.5
  105.3 42.6 all-gather.7
  178.8 37.8 reduce-scatter.2
  219.2 69.4 all-gather.9
  290.2 25.7 all-gather.11
  317.6 26.8 all-gather.13
  352.9 86.7 reduce-scatter.4
where the time goes:
time: 454 us; the launch traced here: 449 us
  waiting for transfers between devices  265 us (58%)
  matrix products  74.5 us (16%)
  other arithmetic  53.9 us (12%)
  local copies, waits for them, and re-layouts  17.9 us (4%)
  between operations  14.8 us (3%)
  starting transfers between devices  13 us (3%)
  blocking collectives  9.9 us (2%)
    reduce_scatter x1, waiting for transfers between devices, shards(): lax.psum_scatter(jnp.dot(block_rows, down_full, preferred_element_type=jn...  86.9 us
    all_gather x1, waiting for transfers between devices, shards(): all_rows = lax.all_gather(normed, 'tp', axis=0, tiled=True)  38.4 us
    reduce_scatter x1, waiting for transfers between devices, shards(): lax.psum_scatter(jnp.dot(block_rows, wo_full, preferred_element_type=jnp....  37.9 us
    all_gather x1, waiting for transfers between devices, side_by_side(): result, at, done = (lax.all_gather(both, axis, axis=dim, tiled=True), 0, [])  33.2 us
    le x8, other arithmetic, attend(): causal = key_pos[None, :] <= query_pos[:, None]  31 us
    all_to_all x1, waiting for transfers between devices, sent_to_all(): return lax.all_to_all(copies, axis, split_axis=0, concat_axis=0, tiled=True)  23.5 us
    dot_general x8, matrix products, attend(): jnp.einsum('qhgd,khd->hgqk', q_four, k_three, preferred_element_type=jnp....  22.5 us
    dot_general x8, matrix products, attend(): jnp.einsum('hgqk,khd->qhgd', probs, v_three, preferred_element_type=jnp.f...  20.4 us
  transfers between devices with their start and end apart: 10, of which 8 were waited for; matrix products, arithmetic and copies ran while one was open for 27% of the time, Pallas kernels for 0%

commit v1 on v0

--- a/solution.py
+++ b/solution.py
@@ -116,7 +116,9 @@
         jnp.mean(attended_wide * attended_wide, axis=1, keepdims=True) + norm_eps
     )
     normed = (attended_wide * inverse_rms * norm_gain.astype(jnp.float32)).astype(jnp.bfloat16)
-    all_rows = lax.all_gather(normed, "tp", axis=0, tiled=True)
+    all_rows = jnp.concatenate(
+        lax.all_to_all(jnp.stack([normed] * lax.axis_size("tp")), "tp", 0, 0), axis=0
+    )
 
     def add_single(weight_piece):
         return add_rows(all_rows, weight_piece)

time: 454 us -> 520 us (1.15)
  waiting for transfers between devices: 265 us -> 319 us
  starting transfers between devices: 13 us -> 20.4 us
    all_to_all x0 -> x1, waiting for transfers between devices: none -> 124 us  [shards(): lax.all_to_all(jnp.stack([normed] * lax.axis_size('tp')), 'tp', 0, 0)]
    all_gather x1 -> x0, waiting for transfers between devices: 38.4 us -> none  [shards(): all_rows = lax.all_gather(normed, 'tp', axis=0, tiled=True)]
    all_to_all x1, waiting for transfers between devices: 23.5 us -> 0.01 us  [sent_to_all(): return lax.all_to_all(copies, axis, split_axis=0, concat_axis=0, tiled=True)]
    reduce_scatter x1, waiting for transfers between devices: 86.9 us -> 108 us  [shards(): lax.psum_scatter(jnp.dot(block_rows, down_full, preferred_element_type=jn...]
    all_gather x1, waiting for transfers between devices: 19.3 us -> 0.02 us  [shards(): down_full = lax.all_gather(down_weight, 'sp', axis=1, tiled=True)]
    all_gather x1, waiting for transfers between devices: 17.6 us -> 0.01 us  [shards(): up_sum = add_single(lax.all_gather(up_weight, 'sp', axis=0, tiled=True))]
    reduce_scatter x1, waiting for transfers between devices: 37.9 us -> 46.7 us  [shards(): lax.psum_scatter(jnp.dot(block_rows, wo_full, preferred_element_type=jnp....]
    all_to_all x0 -> x1, starting transfers between devices: none -> 6.64 us  [shards(): lax.all_to_all(jnp.stack([normed] * lax.axis_size('tp')), 'tp', 0, 0)]
  transfers between devices with their start and end apart: 10 -> 10, of which waited for: 8 -> 5; matrix products, arithmetic and copies ran while one was open for 27% -> 24% of each run, Pallas kernels for 0% -> 0%
where the time goes in v1:
time: 520 us; the launch traced here: 514 us
  waiting for transfers between devices  319 us (61%)
  matrix products  74.5 us (14%)
  other arithmetic  53.1 us (10%)
  local copies, waits for them, and re-layouts  22.2 us (4%)
  starting transfers between devices  20.4 us (4%)
  between operations  14.8 us (3%)
  blocking collectives  9.9 us (2%)
    all_to_all x1, waiting for transfers between devices, shards(): lax.all_to_all(jnp.stack([normed] * lax.axis_size('tp')), 'tp', 0, 0)  124 us
    reduce_scatter x1, waiting for transfers between devices, shards(): lax.psum_scatter(jnp.dot(block_rows, down_full, preferred_element_type=jn...  108 us
    reduce_scatter x1, waiting for transfers between devices, shards(): lax.psum_scatter(jnp.dot(block_rows, wo_full, preferred_element_type=jnp....  46.7 us
    all_gather x1, waiting for transfers between devices, side_by_side(): result, at, done = (lax.all_gather(both, axis, axis=dim, tiled=True), 0, [])  33.1 us
    le x8, other arithmetic, attend(): causal = key_pos[None, :] <= query_pos[:, None]  31 us
    dot_general x8, matrix products, attend(): jnp.einsum('qhgd,khd->hgqk', q_four, k_three, preferred_element_type=jnp....  22.5 us
    dot_general x8, matrix products, attend(): jnp.einsum('hgqk,khd->qhgd', probs, v_three, preferred_element_type=jnp.f...  20.4 us
    dot_general x2, matrix products, add_rows(): return jnp.dot(all_rows, weight_piece, preferred_element_type=jnp.float32)  18.8 us
  transfers between devices with their start and end apart: 10, of which 5 were waited for; matrix products, arithmetic and copies ran while one was open for 24% of the time, Pallas kernels for 0%

profile of v1, /device:TPU:0, one launch (start us, length us, event | category | flops | bytes accessed | tf_op | source)
XLA Modules:
  0.0 514.2 jit_solution(17966744930001208946)
XLA Ops:
  9.2 5.4 %all-to-all-start.1 = ((bf16[128,8,128]{2,0,1:T(8,128)(2,1)}), bf16[128,8,128]{2,0,1:T(8,128)(2,1)S(1)}, u32[]{:S(2)}, u32[]{:S(2)}) async-start(bf16[128,8,128]{2,0,1:T(8,128)(2,1)} %copy.90), calls=%async_computation.1 | async-start | bytes 524288 | tf_op jit(solution)/shard_map/all_to_all | solution.py:68
  16.0 6.1 %all-to-all-done.1 = bf16[128,8,128]{2,0,1:T(8,128)(2,1)S(1)} async-done(((bf16[128,8,128]{2,0,1:T(8,128)(2,1)}), bf16[128,8,128]{2,0,1:T(8,128)(2,1)S(1)}, u32[]{:S(2)}, u32[]{:S(2)}) %all-to-all-start.1) | async-done | bytes 262176 | tf_op jit(solution)/shard_map/all_to_all | solution.py:68
  22.1 9.9 %all_to_all.58 = bf16[128,8,128]{2,0,1:T(8,128)(2,1)S(1)} all-to-all(bf16[128,8,128]{2,0,1:T(8,128)(2,1)S(1)} %copy.88), channel_id=1, replica_groups=mesh['sp'=8,'tp'=16] {'sp'}, dimensions={1} | all-to-all | bytes 524288 | tf_op jit(solution)/shard_map/all_to_all | solution.py:67
  33.9 3.5 all-to-all-start.2
  38.3 2.4 iota_compare_fusion
  42.6 3.4 broadcast_compare_fusion.4
  46.0 4.4 broadcast_compare_fusion.3
  50.4 5.6 %broadcast_compare_fusion.2 = pred[128,10240]{0,1:T(8,128)(4,1)} fusion(s32[128]{0:T(128)S(1)} %get-tuple-element.29, s32[10240]{0:T(1024)S(1)} %iota_add_fusion.2), kind=kLoop, calls=%fused_computation.62 | loop fusion | flops 1310720 | bytes 1352192 | tf_op jit(solution)/shard_map/le | solution.py:44
  56.0 6.4 %broadcast_compare_fusion.1 = pred[128,12288]{0,1:T(8,128)(4,1)} fusion(s32[128]{0:T(128)S(1)} %get-tuple-element.28, s32[12288]{0:T(1024)S(1)} %iota_add_fusion.1), kind=kLoop, calls=%fused_computation.59 | loop fusion | flops 1572864 | bytes 1622528 | tf_op jit(solution)/shard_map/le | solution.py:44
  62.3 6.7 %broadcast_compare_fusion = pred[128,14336]{0,1:T(8,128)(4,1)S(1)} fusion(s32[128]{0:T(128)S(1)} %get-tuple-element.27, s32[14336]{0:T(1024)S(1)} %iota_add_fusion), kind=kLoop, calls=%fused_computation.56 | loop fusion | flops 1835008 | bytes 1892864 | tf_op jit(solution)/shard_map/le | solution.py:44
  70.1 33.1 %all-gather.5.cloned.1.call-done = bf16[16,2048,128]{2,1,0:T(8,128)(2,1)} async-done(((bf16[16,128,128]{2,1,0:T(8,128)(2,1)}), bf16[16,2048,128]{2,1,0:T(8,128)(2,1)}) %all-gather.5.cloned.1.call-update) | async-done | bytes 8388624 | tf_op jit(solution)/shard_map/all_gather | solution.py:12
  123.1 2.2 fusion.87
  126.7 2.1 fusion.47
  130.2 2.7 fusion.88
  134.6 2.5 fusion.50
  137.7 6.9 %fusion.89 = (f32[2,128]{1,0:T(2,128)S(1)}, f32[1,2,128,14336]{2,3,1,0:T(8,128)}) fusion(bf16[14336,128,1]{1,0,2:T(8,128)(2,1)S(1)} %bitcast.230, bf16[128,2,128]{0,2,1:T(8,128)(2,1)S(1)} %bitcast.248, pred[128,14336]{0,1:T(8,128)(4,1)S(1)} %broadcast_compare_fusion), kind=kOutput, calls=%fused_computation.138 | convolution fusion | flops 950533888 | bytes 20251648 | tf_op jit(solution)/shard_map/qhgd,khd->hgqk/dot_general | solution.py:41
  144.6 7.4 %fusion.8 = f32[2,128]{1,0:T(2,128)S(1)} fusion(f32[1,2,128,14336]{2,3,1,0:T(8,128)} %get-tuple-element.47, f32[2,128]{1,0:T(2,128)S(1)} %get-tuple-element.46), kind=kLoop, calls=%fused_computation.16 | loop fusion | flops 7339776 | bytes 14682112 | tf_op jit(solution)/shard_map/reduce_sum | solution.py:48
  152.0 6.9 %fusion.53 = bf16[128,2,128]{2,0,1:T(8,128)(2,1)S(1)} fusion(bf16[14336,128,1]{1,0,2:T(8,128)(2,1)S(1)} %bitcast.229, f32[2,128]{1,0:T(2,128)S(1)} %fusion.8, f32[1,2,128,14336]{2,3,1,0:T(8,128)} %get-tuple-element.47, f32[2,128]{1,0:T(2,128)S(1)} %get-tuple-element.46), kind=kOutput, calls=%fused_computation.79 | convolution fusion | flops 950566912 | bytes 18417664 | tf_op jit(solution)/shard_map/hgqk,khd->qhgd/dot_general | solution.py:49
  158.9 2.2 fusion.74
  161.2 5.2 %fusion.90 = (f32[2,128]{1,0:T(2,128)S(1)}, f32[1,2,128,16384]{2,3,1,0:T(8,128)S(1)}) fusion(bf16[16384,128,1]{1,0,2:T(8,128)(2,1)} %bitcast.228, bf16[128,2,128]{0,2,1:T(8,128)(2,1)S(1)} %bitcast.247, pred[128,16384]{0,1:T(8,128)(4,1)S(1)} %copy-done.2), kind=kOutput, calls=%fused_computation.139 | convolution fusion | flops 1086324480 | bytes 23135232 | tf_op jit(solution)/shard_map/qhgd,khd->hgqk/dot_general | solution.py:41
  166.4 4.4 fusion.6
  170.8 3.2 fusion.56
  174.1 4.5 convolution_convert_fusion.1
  180.1 4.4 all-to-all-start.4
  184.5 46.7 %reduce-scatter.3.cloned.1.call-done = bf16[128,2048]{1,0:T(8,128)(2,1)} async-done(((bf16[1024,2048]{1,0:T(8,128)(2,1)}), bf16[128,2048]{1,0:T(8,128)(2,1)}) %reduce-scatter.3.cloned.1.call-update) | async-done | bytes 524304 | tf_op jit(solution)/shard_map/reduce_scatter | solution.py:107
  232.8 4.3 stack.2
  237.1 6.6 %all-to-all-start.3 = ((bf16[16,128,2048]{2,1,0:T(8,128)(2,1)}), bf16[16,128,2048]{2,1,0:T(8,128)(2,1)}, u32[]{:S(2)}, u32[]{:S(2)}) async-start(bf16[16,128,2048]{2,1,0:T(8,128)(2,1)} %stack.2), calls=%async_computation.4 | async-start | bytes 16777216 | tf_op jit(solution)/shard_map/all_to_all | solution.py:120
  246.6 123.7 %all-to-all-done.3 = bf16[16,128,2048]{2,1,0:T(8,128)(2,1)} async-done(((bf16[16,128,2048]{2,1,0:T(8,128)(2,1)}), bf16[16,128,2048]{2,1,0:T(8,128)(2,1)}, u32[]{:S(2)}, u32[]{:S(2)}) %all-to-all-start.3) | async-done | bytes 8388640 | tf_op jit(solution)/shard_map/all_to_all | solution.py:120
  370.3 9.7 %fusion.91 = f32[2048,448]{0,1:T(8,128)} fusion(bf16[2048,2048]{1,0:T(8,128)(2,1)} %bitcast.94, bf16[2048,448]{0,1:T(8,128)(2,1)} %bitcast.238), kind=kOutput, calls=%fused_computation.140 | convolution fusion | flops 3758096384 | bytes 13893632 | tf_op jit(solution)/shard_map/dot_general | solution.py:54
  380.0 9.1 %multiply_convert_fusion = bf16[2048,448]{0,1:T(8,128)(2,1)S(1)} fusion(f32[2048,448]{0,1:T(8,128)} %fusion.91, bf16[2048,2048]{1,0:T(8,128)(2,1)} %bitcast.94, bf16[2048,448]{0,1:T(8,128)(2,1)} %all-gather.9.cloned.1.call-done), kind=kOutput, calls=%fused_computation.55 | convolution fusion | flops 3763601408 | bytes 15728640 | tf_op jit(solution)/shard_map/dot_general | solution.py:54
  389.1 8.3 %convolution_convert_fusion = bf16[2048,2048]{1,0:T(8,128)(2,1)} fusion(bf16[2048,448]{0,1:T(8,128)(2,1)S(1)} %multiply_convert_fusion, bf16[448,2048]{1,0:T(8,128)(2,1)} %all-gather.11.cloned.1.call-done), kind=kOutput, calls=%fused_computation.34 | convolution fusion | flops 3762290688 | bytes 12058624 | tf_op jit(solution)/shard_map/dot_general | solution.py:132
  397.4 107.8 %reduce-scatter.5.cloned.1.call-done = bf16[128,2048]{1,0:T(8,128)(2,1)} async-done(((bf16[2048,2048]{1,0:T(8,128)(2,1)}), bf16[128,2048]{1,0:T(8,128)(2,1)}) %reduce-scatter.5.cloned.1.call-update) | async-done | bytes 524304 | tf_op jit(solution)/shard_map/reduce_scatter | solution.py:131
  (104 shorter events, 41.7 us)
Async XLA Ops:
  7.2 25.7 %copy-start.7 = (bf16[128,2048]{1,0:T(8,128)(2,1)S(1)}, bf16[128,2048]{1,0:T(8,128)(2,1)}, u32[]{:S(2)}) copy-start(bf16[128,2048]{1,0:T(8,128)(2,1)} %param.10) | copy-start | bytes 1572868
  9.2 12.9 %all-to-all-start.1 = ((bf16[128,8,128]{2,0,1:T(8,128)(2,1)}), bf16[128,8,128]{2,0,1:T(8,128)(2,1)S(1)}, u32[]{:S(2)}, u32[]{:S(2)}) async-start(bf16[128,8,128]{2,0,1:T(8,128)(2,1)} %copy.90), calls=%async_computation.1 | async-start | bytes 524288 | tf_op jit(solution)/shard_map/all_to_all | solution.py:68
  14.6 88.6 %all-gather.5.cloned.1.call-start = ((), (), s32[]{:S(2)}) async-start(), calls=%async_computation.7 | async-start | bytes 8912896 | tf_op jit(solution)/shard_map/all_gather | solution.py:12
  33.9 35.4 %all-to-all-start.2 = ((bf16[128,8,256]{0,2,1:T(8,128)(2,1)}), bf16[128,8,256]{0,2,1:T(8,128)(2,1)S(1)}, u32[]{:S(2)}, u32[]{:S(2)}) async-start(bf16[128,8,256]{0,2,1:T(8,128)(2,1)} %bitcast.8), calls=%async_computation.2 | async-start | bytes 1048576 | tf_op jit(solution)/shard_map/all_to_all | solution.py:65
  37.4 136.7 %all-gather.7.cloned.1.call-start = ((), (), s32[]{:S(2)}) async-start(), calls=%async_computation.8 | async-start | bytes 1114112 | tf_op jit(solution)/shard_map/all_gather | solution.py:105
  38.2 193.0 %reduce-scatter.3.cloned.1.call-start = ((), (), s32[]{:S(2)}) async-start(), calls=%async_computation.9 | async-start | bytes 4718592 | tf_op jit(solution)/shard_map/reduce_scatter | solution.py:107
  105.1 3.5 copy-start
  106.8 1.9 copy-start.15
  111.2 1.1 copy-start.6
  111.2 1.1 copy-start.14
  115.9 1.2 copy-start.5
  115.9 1.2 copy-start.13
  121.7 1.3 copy-start.4
  121.7 1.3 copy-start.12
  128.8 1.4 copy-start.3
  128.8 1.4 copy-start.11
  158.9 2.3 copy-start.2
  158.9 2.3 copy-start.10
  174.1 4.6 copy-start.9
  178.6 5.9 %copy-start.16 = (bf16[2048]{0:T(1024)(128)(2,1)S(1)}, bf16[2048]{0:T(1024)(128)(2,1)}, u32[]{:S(2)}) copy-start(bf16[2048]{0:T(1024)(128)(2,1)} %param.14) | copy-start | bytes 12292
  178.6 52.6 %copy-start.8 = (bf16[128,2048]{1,0:T(8,128)(2,1)S(1)}, bf16[128,2048]{1,0:T(8,128)(2,1)}, u32[]{:S(2)}) copy-start(bf16[128,2048]{1,0:T(8,128)(2,1)} %param.9) | copy-start | bytes 1572868
  180.1 52.7 %all-to-all-start.4 = ((bf16[8,256,448]{1,2,0:T(8,128)(2,1)}), bf16[8,256,448]{1,2,0:T(8,128)(2,1)S(1)}, u32[]{:S(2)}, u32[]{:S(2)}) async-start(bf16[8,256,448]{1,2,0:T(8,128)(2,1)} %broadcast_in_dim.157), calls=%async_computation.5 | async-start | bytes 3670016 | tf_op jit(solution)/shard_map/all_to_all | solution.py:21
  232.5 272.6 %copy-start.1 = (bf16[128,2048]{1,0:T(8,128)(2,1)}, bf16[128,2048]{1,0:T(8,128)(2,1)S(1)}, u32[]{:S(2)}) copy-start(bf16[128,2048]{1,0:T(8,128)(2,1)S(1)} %get-tuple-element.3) | copy-start | bytes 1572868
  237.1 133.2 %all-to-all-start.3 = ((bf16[16,128,2048]{2,1,0:T(8,128)(2,1)}), bf16[16,128,2048]{2,1,0:T(8,128)(2,1)}, u32[]{:S(2)}, u32[]{:S(2)}) async-start(bf16[16,128,2048]{2,1,0:T(8,128)(2,1)} %stack.2), calls=%async_computation.4 | async-start | bytes 16777216 | tf_op jit(solution)/shard_map/all_to_all | solution.py:120
  243.7 136.2 %all-gather.9.cloned.1.call-start = ((), (), s32[]{:S(2)}) async-start(), calls=%async_computation.10 | async-start | bytes 2064384 | tf_op jit(solution)/shard_map/all_gather | solution.py:127
  244.3 144.8 %all-gather.11.cloned.1.call-start = ((), (), s32[]{:S(2)}) async-start(), calls=%async_computation.11 | async-start | bytes 2064384 | tf_op jit(solution)/shard_map/all_gather | solution.py:129
  244.9 260.3 %reduce-scatter.5.cloned.1.call-start = ((), (), s32[]{:S(2)}) async-start(), calls=%async_computation.12 | async-start | bytes 8912896 | tf_op jit(solution)/shard_map/reduce_scatter | solution.py:131
Sparse Core Ops, SparseCore 0:
  33.0 70.1 all-gather.4
  105.3 42.6 all-gather.6
  178.8 52.3 reduce-scatter.2
  245.9 25.1 all-gather.8
  272.7 26.8 all-gather.10
  397.5 107.6 reduce-scatter.4
